TPU v7x, 32 devices: a whole 2x2x4 slice. The times are simulated.
32 devices in a mesh: rows: 8 (over y, x, core), cols: 4 (over z).
Axes of the slice: x: 2, y: 2, z: 4, core: 2. Of those that a mesh axis runs over, the one named last changes fastest.
Arguments:
- projection: float32 [4096, 65536], P('rows', 'cols'), may hold values from -0.09375 to 0.09375
- basis: float32 [128, 65536], P(None, ('cols', 'rows')), may hold values from -6 to 6
Outputs:
- new_block: float32 [16, 65536], P(None, ('cols', 'rows'))
- coefficients: float32 [128, 16], replicated
- factor: float32 [16, 16], replicated
All inputs are finite; a program needn't handle non-finite values.
Results may differ from a plain program's by a relative error of at most 0.0029.
Values sent between devices are 32-bit elements; how exact they have to be, the bound alone decides.
No kernel may reach another device: no remote copies, remote signals or barrier semaphores. Data moves between devices by JAX's collectives and lax.ppermute only.
A program may use at most 64 MiB of HBM per device.

v0:
```python
import jax
import jax.numpy as jnp
from jax import lax
from jax.sharding import PartitionSpec as P

N = 65536
BS = 16


def contract(left, right):
    return lax.dot_general(
        left,
        right,
        (((1,), (1,)), ((), ())),
        precision=lax.Precision.HIGHEST,
        preferred_element_type=jnp.float32,
    )


def matmul(left, right):
    return jnp.dot(left, right, precision=lax.Precision.HIGHEST, preferred_element_type=jnp.float32)


def wide_reduce(values):
    return lax.psum(values, ("rows", "cols"))


def orthogonalize(vectors, image, reducer):
    cross, correlation, self_gram = reducer(
        (contract(vectors, image), contract(vectors, vectors), contract(image, image))
    )
    cross = cross / N
    correlation = correlation / N
    self_gram = self_gram / N
    coeffs = cross + (cross - matmul(correlation, cross))
    gram_matrix = (
        self_gram
        - matmul(cross.T, coeffs)
        - matmul(coeffs.T, cross)
        + matmul(coeffs.T, matmul(correlation, coeffs))
    )
    image_two = image - matmul(coeffs.T, vectors)
    factor = jnp.linalg.cholesky(gram_matrix)
    new_block = jax.scipy.linalg.solve_triangular(factor, image_two, lower=True)
    return (new_block, coeffs, factor)


def local(projection, basis):
    current = basis[basis.shape[0] - BS :]
    partial_value = contract(lax.all_gather(current, "rows", axis=1, tiled=True), projection)
    projected = lax.psum(partial_value, "cols")
    image = matmul(projected, projection)
    adjoint = lax.psum_scatter(image, "rows", scatter_dimension=1, tiled=True)
    return orthogonalize(basis, adjoint, wide_reduce)


def solution(mesh):
    placed = (P("rows", "cols"), P(None, ("cols", "rows")))
    return jax.shard_map(
        local,
        mesh=mesh,
        in_specs=placed,
        out_specs=(P(None, ("cols", "rows")), P(), P()),
        check_vma=False,
    )
```

profile of v0, /device:TPU:1, one launch (start us, length us, event | category | flops | bytes accessed | tf_op | source)
XLA Modules:
  0.0 251.2 jit_solution(9730778745734969005)
XLA Ops:
  8.0 0.0 all-gather.2.cloned.1.call-start
  8.0 1.6 slice.15
  9.6 0.0 all-gather.2.cloned.1.call-update
  9.6 0.0 copy-start
  9.7 0.0 reduce-scatter.2.cloned.1.call-start
  9.7 27.4 %all-gather.2.cloned.1.call-done = f32[16,16384]{1,0:T(8,128)} async-done(((f32[16,2048]{1,0:T(8,128)}), f32[16,16384]{1,0:T(8,128)}) %all-gather.2.cloned.1.call-update) | async-done | bytes 1048592 | tf_op jit(solution)/shard_map/all_gather | solution.py:50
  37.1 33.1 %fusion.19 = f32[16,512]{1,0:T(8,128)S(1)} fusion(f32[16,16384]{1,0:T(8,128)} %all-gather.2.cloned.1.call-done, f32[512,16384]{1,0:T(8,128)} %param.2), kind=kOutput, calls=%fused_computation.32 | convolution fusion | flops 1610612736 | bytes 34635776 | tf_op jit(solution)/shard_map/dot_general | solution.py:11
  70.3 15.2 %psum.28 = f32[16,512]{1,0:T(8,128)S(1)} all-reduce(f32[16,512]{1,0:T(8,128)S(1)} %fusion.19), channel_id=1, replica_groups=mesh['rows'=8,'cols'=4] {'cols'}, use_global_device_ids=true, to_apply=%region_0.0 | all-reduce | flops 8192 | bytes 65536 | tf_op jit(solution)/shard_map/psum | solution.py:51
  85.5 20.3 %fusion.20 = f32[16,16384]{1,0:T(8,128)} fusion(f32[16,512]{1,0:T(8,128)S(1)} %psum.28, f32[512,16384]{1,0:T(8,128)} %param.2), kind=kOutput, calls=%fused_computation.33 | convolution fusion | flops 1610612736 | bytes 34635776 | tf_op jit(solution)/shard_map/dot_general | solution.py:21
  105.8 0.0 reduce-scatter.2.cloned.1.call-update
  105.9 0.0 all-reduce.3.cloned.1.call-start
  105.9 0.0 copy-done
  105.9 1.6 fusion.22
  107.5 0.0 all-reduce.3.cloned.1.call-update
  107.6 34.7 %reduce-scatter.2.cloned.1.call-done = f32[16,2048]{1,0:T(8,128)} async-done(((f32[16,16384]{1,0:T(8,128)}), f32[16,2048]{1,0:T(8,128)}) %reduce-scatter.2.cloned.1.call-update) | async-done | bytes 131088 | tf_op jit(solution)/shard_map/reduce_scatter | solution.py:53
  142.3 1.8 convolution_bitcast_fusion
  144.1 1.2 fusion.21
  145.3 39.0 %all-reduce = (f32[128,16]{0,1:T(8,128)S(1)}, f32[16,16]{0,1:T(8,128)S(1)}) all-reduce(f32[128,16]{0,1:T(8,128)S(1)} %convolution_bitcast_fusion, f32[16,16]{0,1:T(8,128)S(1)} %fusion.21), channel_id=1, replica_groups=mesh['rows'=8,'cols'=4] {'rows','cols'}, use_global_device_ids=true, to_apply=%region_3.0 | all-reduce | flops 2304 | bytes 18432 | tf_op jit(solution)/shard_map/psum | solution.py:25
  184.4 49.6 %all-reduce.3.cloned.1.call-done = f32[128,128]{1,0:T(8,128)} async-done(((f32[128,128]{1,0:T(8,128)}), f32[128,128]{1,0:T(8,128)}) %all-reduce.3.cloned.1.call-update) | async-done | bytes 65552 | tf_op jit(solution)/shard_map/psum | solution.py:25
  233.9 1.0 fusion
  235.0 0.0 copy-start.1
  235.0 0.1 convolution_subtract_fusion.3
  235.1 0.1 convolution_subtract_fusion.2
  235.3 1.0 fusion.1
  236.3 0.2 convolution_add_fusion
  236.5 0.1 copy.9
  236.6 1.5 cholesky.16
  238.1 0.6 compare_reduce_fusion
  238.8 1.2 select_bitcast_fusion
  240.0 1.2 custom-call.7
  241.3 1.5 convolution_subtract_fusion
  242.8 1.0 fusion.6
  (3 shorter events, 0.0 us)
Async XLA Ops:
  8.0 29.1 %all-gather.2.cloned.1.call-start = ((), (), s32[]{:S(2)}) async-start(), calls=%async_computation.1 | async-start | bytes 1179648 | tf_op jit(solution)/shard_map/all_gather | solution.py:50
  9.6 96.3 %copy-start = (f32[128,2048]{1,0:T(8,128)S(1)}, f32[128,2048]{1,0:T(8,128)}, u32[]{:S(2)}) copy-start(f32[128,2048]{1,0:T(8,128)} %param.3) | copy-start | bytes 3145732
  9.7 132.6 %reduce-scatter.2.cloned.1.call-start = ((), (), s32[]{:S(2)}) async-start(), calls=%async_computation.2 | async-start | bytes 1179648 | tf_op jit(solution)/shard_map/reduce_scatter | solution.py:53
  105.9 128.1 %all-reduce.3.cloned.1.call-start = ((), (), s32[]{:S(2)}) async-start(), calls=%async_computation.3 | async-start | bytes 131072 | tf_op jit(solution)/shard_map/psum | solution.py:25
  235.0 8.8 %copy-start.1 = (f32[128,16]{0,1:T(8,128)}, f32[128,16]{0,1:T(8,128)S(1)}, u32[]{:S(2)}) copy-start(f32[128,16]{0,1:T(8,128)S(1)} %fusion) | copy-start | bytes 24580
Sparse Core Ops, SparseCore 0:
  11.3 25.8 all-gather.1
  106.0 36.2 reduce-scatter.1
Sparse Core Ops, SparseCore 1:
  112.5 121.4 all-reduce.2
where the time goes:
time: 252 us; the launch traced here: 251 us
  waiting for transfers between devices  112 us (44%)
  matrix products  63.2 us (25%)
  blocking collectives  54.3 us (22%)
  between operations  15.6 us (6%)
  other arithmetic  4.65 us (2%)
    psum x1, waiting for transfers between devices, wide_reduce(): return lax.psum(values, ('rows', 'cols'))  49.6 us
    psum x1, blocking collectives, wide_reduce(): return lax.psum(values, ('rows', 'cols'))  39 us
    dot_general x4, matrix products, contract(): lax.dot_general(left, right, (((1,), (1,)), ((), ())), precision=lax.Prec...  37.8 us
    reduce_scatter x1, waiting for transfers between devices, local(): adjoint = lax.psum_scatter(image, 'rows', scatter_dimension=1, tiled=True)  34.7 us
    all_gather x1, waiting for transfers between devices, local(): lax.all_gather(current, 'rows', axis=1, tiled=True)  27.4 us
    dot_general x7, matrix products, matmul(): jnp.dot(left, right, precision=lax.Precision.HIGHEST, preferred_element_t...  24.4 us
    psum x1, blocking collectives, local(): projected = lax.psum(partial_value, 'cols')  15.2 us
  transfers between devices with their start and end apart: 3, of which 3 were waited for; matrix products, arithmetic and copies ran while one was open for 2% of the time, Pallas kernels for 0%

commit v1 on v0

--- a/solution.py
+++ b/solution.py
@@ -5,6 +5,32 @@
 
 N = 65536
 BS = 16
+
+
+def measure_lots_all(my_data, in_dim):
+    my_data = jnp.moveaxis(my_data, 0, in_dim)
+    z1 = my_data.shape
+    return my_data.reshape(*z1[:in_dim], z1[in_dim] * z1[in_dim + 1], *z1[in_dim + 2 :])
+
+
+def form_the_pools(buf, peer_axis, dim_no):
+    cores_n = lax.axis_size(peer_axis)
+    fields = [(c, (c + 1) % cores_n) for c in range(cores_n)]
+    rows = [(u, no) for no, u in fields]
+    top, all_rows = ([], [])
+    j = 0
+    while j < cores_n - 1:
+        if j % 2 == 0:
+            top.append(lax.ppermute(top[-1] if top else buf, perm=fields, axis_name=peer_axis))
+        else:
+            all_rows.append(
+                lax.ppermute(all_rows[-1] if all_rows else buf, axis_name=peer_axis, perm=rows)
+            )
+        j = j + 1
+    latest = jnp.stack([*top[::-1], buf, *all_rows])
+    later = lax.axis_index(peer_axis) - len(top)
+    latest = latest[(jnp.arange(cores_n) - later) % cores_n]
+    return measure_lots_all(latest, dim_no)
 
 
 def contract(left, right):
@@ -47,7 +73,7 @@
 
 def local(projection, basis):
     current = basis[basis.shape[0] - BS :]
-    partial_value = contract(lax.all_gather(current, "rows", axis=1, tiled=True), projection)
+    partial_value = contract(form_the_pools(current, "rows", 1), projection)
     projected = lax.psum(partial_value, "cols")
     image = matmul(projected, projection)
     adjoint = lax.psum_scatter(image, "rows", scatter_dimension=1, tiled=True)

time: 252 us -> 248 us (0.984)
  waiting for transfers between devices: 112 us -> 98 us
  starting transfers between devices: 0.12 us -> 10.2 us
    all_gather x1 -> x0, waiting for transfers between devices: 27.4 us -> none  [local(): lax.all_gather(current, 'rows', axis=1, tiled=True)]
    ppermute x0 -> x7, waiting for transfers between devices: none -> 11.2 us  [the longest x3 6.5 us: form_the_pools(): lax.ppermute(all_rows[-1] if all_rows else buf, axis_name=peer_axis, perm...]
    ppermute x0 -> x7, starting transfers between devices: none -> 9.98 us  [the longest x4 9.98 us: form_the_pools(): lax.ppermute(top[-1] if top else buf, perm=fields, axis_name=peer_axis)]
  transfers between devices with their start and end apart: 3 -> 9, of which waited for: 3 -> 9; matrix products, arithmetic and copies ran while one was open for 2% -> 2% of each run, Pallas kernels for 0% -> 0%
where the time goes in v1:
time: 248 us; the launch traced here: 247 us
  waiting for transfers between devices  98 us (40%)
  matrix products  61 us (25%)
  blocking collectives  54.9 us (22%)
  between operations  15.6 us (6%)
  starting transfers between devices  10.2 us (4%)
  other arithmetic  4.67 us (2%)
  local copies, waits for them, and re-layouts  2.74 us (1%)
    psum x1, waiting for transfers between devices, wide_reduce(): return lax.psum(values, ('rows', 'cols'))  49.5 us
    psum x1, blocking collectives, wide_reduce(): return lax.psum(values, ('rows', 'cols'))  39.1 us
    reduce_scatter x1, waiting for transfers between devices, local(): adjoint = lax.psum_scatter(image, 'rows', scatter_dimension=1, tiled=True)  37.1 us
    dot_general x4, matrix products, contract(): lax.dot_general(left, right, (((1,), (1,)), ((), ())), precision=lax.Prec...  35.6 us
    dot_general x7, matrix products, matmul(): jnp.dot(left, right, precision=lax.Precision.HIGHEST, preferred_element_t...  24.4 us
    psum x1, blocking collectives, local(): projected = lax.psum(partial_value, 'cols')  15.9 us
    ppermute x4, starting transfers between devices, form_the_pools(): lax.ppermute(top[-1] if top else buf, perm=fields, axis_name=peer_axis)  9.98 us
    ppermute x3, waiting for transfers between devices, form_the_pools(): lax.ppermute(all_rows[-1] if all_rows else buf, axis_name=peer_axis, perm...  6.5 us
  transfers between devices with their start and end apart: 9, of which 9 were waited for; matrix products, arithmetic and copies ran while one was open for 2% of the time, Pallas kernels for 0%

profile of v1, /device:TPU:1, one launch (start us, length us, event | category | flops | bytes accessed | tf_op | source)
XLA Modules:
  0.0 247.2 jit_solution(10270068916866925882)
XLA Ops:
  8.0 0.9 slice.15
  9.0 2.6 %collective-permute-start = (f32[16,2048]{1,0:T(8,128)S(1)}, f32[16,2048]{1,0:T(8,128)S(1)}, u32[]{:S(2)}, u32[]{:S(2)}) collective-permute-start(f32[16,2048]{1,0:T(8,128)S(1)} %slice.15), channel_id=1, source_target_pairs={{0,4},{4,8},{8,12},{12,16},{16,20},{20,24},{24,28},{28,0},{1,5},{5... | collective-permute-start | bytes 393224 | tf_op jit(solution)/shard_map/ppermute | solution.py:24
  11.6 1.9 collective-permute-done
  13.6 2.4 collective-permute-start.1
  16.0 1.9 collective-permute-done.1
  17.9 2.4 collective-permute-start.2
  20.4 1.3 collective-permute-done.4
  21.7 0.6 collective-permute-done.2
  22.3 2.4 collective-permute-start.3
  24.8 1.7 collective-permute-done.5
  26.6 0.2 collective-permute-done.3
  26.9 0.9 bitcast_dynamic-update-slice_fusion.3
  27.8 3.4 %collective-permute-done.6 = f32[16,2048]{1,0:T(8,128)S(1)} collective-permute-done((f32[16,2048]{1,0:T(8,128)S(1)}, f32[16,2048]{1,0:T(8,128)S(1)}, u32[]{:S(2)}, u32[]{:S(2)}) %collective-permute-start.6) | collective-permute-done | bytes 131104 | tf_op jit(solution)/shard_map/ppermute | solution.py:27
  31.3 0.6 gather_fusion
  32.0 31.0 %fusion.21 = f32[16,512]{1,0:T(8,128)S(1)} fusion(f32[16,16384]{1,0:T(8,128)S(1)} %bitcast.50, f32[512,16384]{1,0:T(8,128)} %param.2), kind=kOutput, calls=%fused_computation.48 | convolution fusion | flops 1610612736 | bytes 34635776 | tf_op jit(solution)/shard_map/dot_general | solution.py:37
  63.0 15.9 %psum.28 = f32[16,512]{1,0:T(8,128)S(1)} all-reduce(f32[16,512]{1,0:T(8,128)S(1)} %fusion.21), channel_id=1, replica_groups=mesh['rows'=8,'cols'=4] {'cols'}, use_global_device_ids=true, to_apply=%region_0.1 | all-reduce | flops 8192 | bytes 65536 | tf_op jit(solution)/shard_map/psum | solution.py:77
  78.8 20.3 %fusion.22 = f32[16,16384]{1,0:T(8,128)} fusion(f32[16,512]{1,0:T(8,128)S(1)} %psum.28, f32[512,16384]{1,0:T(8,128)} %param.2), kind=kOutput, calls=%fused_computation.49 | convolution fusion | flops 1610612736 | bytes 34635776 | tf_op jit(solution)/shard_map/dot_general | solution.py:47
  99.2 0.2 all-reduce.3.cloned.1.call-start
  99.4 1.6 fusion.24
  101.1 37.1 %reduce-scatter.2.cloned.1.call-done = f32[16,2048]{1,0:T(8,128)} async-done(((f32[16,16384]{1,0:T(8,128)}), f32[16,2048]{1,0:T(8,128)}) %reduce-scatter.2.cloned.1.call-update) | async-done | bytes 131088 | tf_op jit(solution)/shard_map/reduce_scatter | solution.py:79
  138.2 1.8 convolution_bitcast_fusion
  140.0 1.2 fusion.23
  141.3 39.1 %all-reduce = (f32[128,16]{0,1:T(8,128)S(1)}, f32[16,16]{0,1:T(8,128)S(1)}) all-reduce(f32[128,16]{0,1:T(8,128)S(1)} %convolution_bitcast_fusion, f32[16,16]{0,1:T(8,128)S(1)} %fusion.23), channel_id=1, replica_groups=mesh['rows'=8,'cols'=4] {'rows','cols'}, use_global_device_ids=true, to_apply=%region_3.4 | all-reduce | flops 2304 | bytes 18432 | tf_op jit(solution)/shard_map/psum | solution.py:51
  180.3 49.5 %all-reduce.3.cloned.1.call-done = f32[128,128]{1,0:T(8,128)} async-done(((f32[128,128]{1,0:T(8,128)}), f32[128,128]{1,0:T(8,128)}) %all-reduce.3.cloned.1.call-update) | async-done | bytes 65552 | tf_op jit(solution)/shard_map/psum | solution.py:51
  229.9 1.0 fusion
  231.2 1.0 fusion.1
  232.6 1.5 cholesky.16
  234.1 0.6 compare_reduce_fusion
  234.7 1.2 select_bitcast_fusion
  236.0 1.2 custom-call.7
  237.2 1.5 convolution_subtract_fusion
  238.7 1.0 fusion.6
  (26 shorter events, 0.9 us)
Async XLA Ops:
  8.0 130.2 %reduce-scatter.2.cloned.1.call-start = ((), (), s32[]{:S(2)}) async-start(), calls=%async_computation.1 | async-start | bytes 1179648 | tf_op jit(solution)/shard_map/reduce_scatter | solution.py:79
  9.0 4.6 %collective-permute-start = (f32[16,2048]{1,0:T(8,128)S(1)}, f32[16,2048]{1,0:T(8,128)S(1)}, u32[]{:S(2)}, u32[]{:S(2)}) collective-permute-start(f32[16,2048]{1,0:T(8,128)S(1)} %slice.15), channel_id=1, source_target_pairs={{0,4},{4,8},{8,12},{12,16},{16,20},{20,24},{24,28},{28,0},{1,5},{5... | collective-permute-start | bytes 393224 | tf_op jit(solution)/shard_map/ppermute | solution.py:24
  13.6 4.4 %collective-permute-start.1 = (f32[16,2048]{1,0:T(8,128)S(1)}, f32[16,2048]{1,0:T(8,128)S(1)}, u32[]{:S(2)}, u32[]{:S(2)}) collective-permute-start(f32[16,2048]{1,0:T(8,128)S(1)} %collective-permute-done), channel_id=1, source_target_pairs={{0,4},{4,8},{8,12},{12,16},{16,20},{20,24},{24,28},{28,0},{1,5},{5... | collective-permute-start | bytes 393224 | tf_op jit(solution)/shard_map/ppermute | solution.py:24
  16.0 5.7 %collective-permute-start.4 = (f32[16,2048]{1,0:T(8,128)S(1)}, f32[16,2048]{1,0:T(8,128)S(1)}, u32[]{:S(2)}, u32[]{:S(2)}) collective-permute-start(f32[16,2048]{1,0:T(8,128)S(1)} %slice.15), channel_id=1, source_target_pairs={{4,0},{8,4},{12,8},{16,12},{20,16},{24,20},{28,24},{0,28},{5,1},{9... | collective-permute-start | bytes 393224 | tf_op jit(solution)/shard_map/ppermute | solution.py:27
  17.9 4.4 %collective-permute-start.2 = (f32[16,2048]{1,0:T(8,128)S(1)}, f32[16,2048]{1,0:T(8,128)S(1)}, u32[]{:S(2)}, u32[]{:S(2)}) collective-permute-start(f32[16,2048]{1,0:T(8,128)S(1)} %collective-permute-done.1), channel_id=1, source_target_pairs={{0,4},{4,8},{8,12},{12,16},{16,20},{20,24},{24,28},{28,0},{1,5},{5... | collective-permute-start | bytes 393224 | tf_op jit(solution)/shard_map/ppermute | solution.py:24
  21.7 4.8 %collective-permute-start.5 = (f32[16,2048]{1,0:T(8,128)S(1)}, f32[16,2048]{1,0:T(8,128)S(1)}, u32[]{:S(2)}, u32[]{:S(2)}) collective-permute-start(f32[16,2048]{1,0:T(8,128)S(1)} %collective-permute-done.4), channel_id=1, source_target_pairs={{4,0},{8,4},{12,8},{16,12},{20,16},{24,20},{28,24},{0,28},{5,1},{9... | collective-permute-start | bytes 393224 | tf_op jit(solution)/shard_map/ppermute | solution.py:27
  22.3 4.4 %collective-permute-start.3 = (f32[16,2048]{1,0:T(8,128)S(1)}, f32[16,2048]{1,0:T(8,128)S(1)}, u32[]{:S(2)}, u32[]{:S(2)}) collective-permute-start(f32[16,2048]{1,0:T(8,128)S(1)} %collective-permute-done.2), channel_id=1, source_target_pairs={{0,4},{4,8},{8,12},{12,16},{16,20},{20,24},{24,28},{28,0},{1,5},{5... | collective-permute-start | bytes 393224 | tf_op jit(solution)/shard_map/ppermute | solution.py:24
  26.6 4.7 %collective-permute-start.6 = (f32[16,2048]{1,0:T(8,128)S(1)}, f32[16,2048]{1,0:T(8,128)S(1)}, u32[]{:S(2)}, u32[]{:S(2)}) collective-permute-start(f32[16,2048]{1,0:T(8,128)S(1)} %collective-permute-done.5), channel_id=1, source_target_pairs={{4,0},{8,4},{12,8},{16,12},{20,16},{24,20},{28,24},{0,28},{5,1},{9... | collective-permute-start | bytes 393224 | tf_op jit(solution)/shard_map/ppermute | solution.py:27
  32.0 67.5 %copy-start = (f32[128,2048]{1,0:T(8,128)S(1)}, f32[128,2048]{1,0:T(8,128)}, u32[]{:S(2)}) copy-start(f32[128,2048]{1,0:T(8,128)} %param.3) | copy-start | bytes 3145732
  99.2 130.7 %all-reduce.3.cloned.1.call-start = ((), (), s32[]{:S(2)}) async-start(), calls=%async_computation.2 | async-start | bytes 131072 | tf_op jit(solution)/shard_map/psum | solution.py:51
  230.9 8.8 %copy-start.1 = (f32[128,16]{0,1:T(8,128)}, f32[128,16]{0,1:T(8,128)S(1)}, u32[]{:S(2)}) copy-start(f32[128,16]{0,1:T(8,128)S(1)} %fusion) | copy-start | bytes 24580
Sparse Core Ops, SparseCore 0:
  99.3 38.8 reduce-scatter.1
Sparse Core Ops, SparseCore 1:
  105.8 124.0 all-reduce.2
